TPU v7x, 32 devices: a whole 2x2x4 slice. The times are simulated.
32 devices in a mesh: dp: 8 (over z, x), tensor: 4 (over y, core).
Axes of the slice: x: 2, y: 2, z: 4, core: 2. Of those that a mesh axis runs over, the one named last changes fastest.
Arguments:
- tokens: bfloat16 [16, 128, 2048], P('dp'), may hold values from -6 to 6
- cotangent: bfloat16 [16, 128, 2048], P('dp'), may hold values from -6 to 6
- routes: int32 [16, 128, 4], P('dp'), may hold values from 0 to 5, as said below
- gates: bfloat16 [16, 128, 4], P('dp'), may hold values from 0.099609375 to 0.5
- lengths: int32 [16], P('dp'), may hold values from 64 to 128, as said below
- deal: int32 [16], replicated, may hold values from 0 to 15, as said below
- norm1_gain: float32 [2048], P('dp'), may hold values from 0.1 to 1.9
- q_weight: float32 [2048, 2048], P('dp', 'tensor'), may hold values from -0.125 to 0.125
- q_bias: float32 [16, 128], P('tensor', 'dp'), may hold values from -3 to 3
- k_weight: float32 [2048, 2048], P('dp', 'tensor'), may hold values from -0.125 to 0.125
- v_weight: float32 [2048, 2048], P('dp', 'tensor'), may hold values from -0.125 to 0.125
- v_bias: float32 [16, 128], P('tensor', 'dp'), may hold values from -3 to 3
- o_weight: float32 [2048, 2048], P('tensor', 'dp'), may hold values from -0.75 to 0.75
- norm2_gain: float32 [2048], P('dp'), may hold values from 0.1 to 1.9
- expert_gate: float32 [6, 2048, 1408], P(None, 'dp', 'tensor'), may hold values from -0.125 to 0.125
- expert_up: float32 [6, 2048, 1408], P(None, 'dp', 'tensor'), may hold values from -0.125 to 0.125
- expert_down: float32 [6, 1408, 2048], P(None, 'tensor', 'dp'), may hold values from -0.21875 to 0.21875
- shared_gate: float32 [2048, 5632], P('dp', 'tensor'), may hold values from -0.125 to 0.125
- shared_up: float32 [2048, 5632], P('dp', 'tensor'), may hold values from -0.125 to 0.125
- shared_down: float32 [5632, 2048], P('tensor', 'dp'), may hold values from -0.109375 to 0.109375
- shared_switch: float32 [2048], P('dp'), may hold values from -0.125 to 0.125
Outputs:
- output: float32 [16, 128, 2048], P('dp', None, 'tensor')
- tokens_grad: float32 [16, 128, 2048], P('dp', None, 'tensor')
- norm1_gain_grad: float32 [2048], P('dp')
- q_weight_grad: float32 [2048, 2048], P('dp', 'tensor')
- q_bias_grad: float32 [16, 128], P('tensor', 'dp')
- k_weight_grad: float32 [2048, 2048], P('dp', 'tensor')
- v_weight_grad: float32 [2048, 2048], P('dp', 'tensor')
- v_bias_grad: float32 [16, 128], P('tensor', 'dp')
- o_weight_grad: float32 [2048, 2048], P('tensor', 'dp')
- norm2_gain_grad: float32 [2048], P('dp')
- expert_gate_grad: float32 [6, 2048, 1408], P(None, 'dp', 'tensor')
- expert_up_grad: float32 [6, 2048, 1408], P(None, 'dp', 'tensor')
- expert_down_grad: float32 [6, 1408, 2048], P(None, 'tensor', 'dp')
- shared_gate_grad: float32 [2048, 5632], P('dp', 'tensor')
- shared_up_grad: float32 [2048, 5632], P('dp', 'tensor')
- shared_down_grad: float32 [5632, 2048], P('tensor', 'dp')
- shared_switch_grad: float32 [2048], P('dp')
Inputs may be any that keep to these rules, and one draw needn't show every extreme that they name: Sequences 2i and 2i+1 are given on dp index i. The two sequences dealt to one dp index have lengths adding up to exactly 192. `deal`: dealt slot 2i holds sequence 2i; the odd sequences move by one common rotation of the dp indices: slot 2i+1 holds sequence 2((i - r) mod the number of dp indices) + 1, for one r of the draw. `routes`: each row names 4 different experts. Among the 192 real tokens dealt to one dp index, every expert is named by exactly 128 tokens. Rows past a sequence's length hold valid ids too.
All inputs are finite; a program needn't handle non-finite values.
Results may differ from a plain program's by a relative error of at most 0.013.
The roundings to bfloat16 on the way count: a program that leaves them out, or rounds other values in their place, can miss the bound.
Values may be sent and summed in bfloat16 or wider, within the bound.
A program may use at most 256 MiB of HBM per device.

v0:
```python
from functools import partial
import jax
import jax.numpy as jnp
from jax import lax
from jax.sharding import PartitionSpec as P

HEAD_DIM = 128
EPSILON = 1e-06
NEGATIVE = -1e30
LANES = 128
BF16 = jnp.bfloat16
F32 = jnp.float32
ALL = ("dp", "tensor")


def normalize(values, gain):
    return values * lax.rsqrt(jnp.mean(values * values, axis=-1, keepdims=True) + EPSILON) * gain


def nt(left, right):
    return lax.dot_general(left, right, (((1,), (1,)), ((), ())), preferred_element_type=F32)


def tn(left, right):
    return lax.dot_general(left, right, (((0,), (0,)), ((), ())), preferred_element_type=F32)


def nn(left, right):
    return lax.dot_general(left, right, (((1,), (0,)), ((), ())), preferred_element_type=F32)


def gather_all(value):
    return lax.all_gather(value, ALL, axis=0, tiled=True)


def scatter_all(value):
    return lax.psum_scatter(value, ALL, scatter_dimension=0, tiled=True)


def exchange_dp(value):
    return lax.all_to_all(value, "dp", 0, 0, tiled=False)


def per_device(
    tokens,
    cotangent,
    routes,
    gates,
    lengths,
    deal,
    norm1_gain,
    q_weight,
    q_bias,
    k_weight,
    v_weight,
    v_bias,
    o_weight,
    norm2_gain,
    expert_gate,
    expert_up,
    expert_down,
    shared_gate,
    shared_up,
    shared_down,
    shared_switch,
):
    n_dp = lax.axis_size("dp")
    n_tensor = lax.axis_size("tensor")
    place = lax.axis_index("dp")
    member = lax.axis_index("tensor")
    seqs, span, width = tokens.shape
    rows = seqs * span
    shard = rows // n_tensor
    experts, slice_d, expert_cols = expert_gate.shape
    shared_cols = shared_gate.shape[1]
    head_cols = q_weight.shape[1]
    heads = head_cols // HEAD_DIM

    def own_rows(value):
        return lax.dynamic_slice_in_dim(value, member * shard, shard, 0)

    valid = (jnp.arange(span)[None, :] < lengths[:, None]).reshape(rows, 1)
    dense = jnp.zeros((seqs, span, LANES), F32)
    for rank in range(routes.shape[-1]):
        hit = routes[..., rank, None] == jnp.arange(LANES)
        dense = dense + jnp.where(hit, gates[..., rank, None].astype(F32), 0.0)
    dense = dense.reshape(rows, LANES).astype(BF16)
    cot = jnp.where(valid, cotangent.reshape(rows, width), 0).astype(BF16)
    cot_packed = gather_all(own_rows(jnp.concatenate([cot, dense], axis=1)))
    small = jnp.concatenate(
        [norm1_gain, norm2_gain, shared_switch, q_bias.reshape(-1), v_bias.reshape(-1)]
    ).astype(BF16)
    small = lax.all_gather(small[None, :], "dp", axis=0, tiled=True)
    gain_one = small[:, :slice_d].reshape(-1).astype(F32)
    gain_two = small[:, slice_d : 2 * slice_d].reshape(-1).astype(F32)
    switch = small[:, 2 * slice_d : 3 * slice_d].reshape(1, -1)
    piece = q_bias.shape[1]

    def whole_bias(start):
        part = small[:, start : start + heads * piece].reshape(n_dp, heads, piece)
        return part.transpose(1, 0, 2).reshape(-1).astype(F32)

    bias_q = whole_bias(3 * slice_d)
    bias_v = whole_bias(3 * slice_d + heads * piece)
    attn_weights = jnp.concatenate(
        [
            q_weight.astype(BF16),
            k_weight.astype(BF16),
            v_weight.astype(BF16),
            o_weight.T.astype(BF16),
        ],
        axis=1,
    )
    attn_weights = lax.all_gather(attn_weights, "dp", axis=0, tiled=True)
    weight_qkv = attn_weights[:, : 3 * head_cols]
    weight_o = attn_weights[:, 3 * head_cols :]

    def by_unit(expert_part, shared_part):
        return jnp.concatenate(
            [
                expert_part.astype(BF16).reshape(n_dp, -1, slice_d),
                shared_part.astype(BF16).reshape(n_dp, -1, slice_d),
            ],
            axis=1,
        )

    gate_sent = by_unit(
        expert_gate.astype(BF16).transpose(0, 2, 1).reshape(-1, slice_d), shared_gate.astype(BF16).T
    )
    up_sent = by_unit(
        expert_up.astype(BF16).transpose(0, 2, 1).reshape(-1, slice_d), shared_up.astype(BF16).T
    )
    down_sent = by_unit(expert_down.reshape(-1, slice_d), shared_down)
    arrived = exchange_dp(jnp.stack([gate_sent, up_sent, down_sent], axis=1))
    units = arrived.shape[2]
    routed = experts * expert_cols // n_dp
    arrived = arrived.transpose(1, 2, 0, 3).reshape(3, units, width)
    gate_units, up_units, down_units = (arrived[0], arrived[1], arrived[2])
    inputs = tokens.reshape(rows, width).astype(F32)
    inputs_own = own_rows(inputs)
    normed_one = normalize(inputs, gain_one).astype(BF16)
    projected = nn(normed_one, weight_qkv)
    head_shape = (seqs, span, heads, HEAD_DIM)
    queries = (projected[:, :head_cols] + bias_q).astype(BF16).reshape(head_shape)
    keys = projected[:, head_cols : 2 * head_cols].astype(BF16).reshape(head_shape)
    values = (projected[:, 2 * head_cols :] + bias_v).astype(BF16).reshape(head_shape)
    order = jnp.arange(span)
    causal = order[None, :] <= order[:, None]
    scale = HEAD_DIM ** (-0.5)
    scores = jnp.einsum("bqhd,bkhd->bhqk", queries, keys, preferred_element_type=F32) * scale
    scores = jnp.where(causal, scores, NEGATIVE)
    top = jnp.max(scores, axis=-1, keepdims=True)
    powers = jnp.exp(scores - top)
    probs = powers / jnp.sum(powers, axis=-1, keepdims=True)
    probs_low = probs.astype(BF16)
    attended = (
        jnp.einsum("bhqk,bkhd->bqhd", probs_low, values, preferred_element_type=F32)
        .reshape(rows, -1)
        .astype(BF16)
    )
    attn_part = nt(attended, weight_o)
    middle = inputs_own + lax.psum_scatter(attn_part, "tensor", scatter_dimension=0, tiled=True)
    normed_two = gather_all(normalize(middle, gain_two).astype(BF16))
    cot_all = cot_packed[:, :width]
    route_share = cot_packed[:, width : width + LANES]
    unit_expert = (place * routed + jnp.arange(routed)) // expert_cols
    picks = (jnp.arange(LANES)[:, None] == unit_expert[None, :]).astype(BF16)
    gate_logit = nt(normed_two, switch)
    switch_gate = jax.nn.sigmoid(gate_logit)
    share = jnp.concatenate(
        [
            nn(route_share, picks),
            jnp.broadcast_to(switch_gate, (switch_gate.shape[0], units - routed)),
        ],
        axis=1,
    )
    gate_act = nt(normed_two, gate_units)
    up_act = nt(normed_two, up_units)
    logistic = jax.nn.sigmoid(gate_act)
    silu = gate_act * logistic
    inner = (silu * up_act).astype(BF16).astype(F32)
    inner_share = (inner * share).astype(BF16)
    mixed = nn(inner_share, down_units).astype(BF16)
    mixed = lax.psum_scatter(mixed, "dp", scatter_dimension=0, tiled=True)
    mixed = lax.psum_scatter(mixed, "tensor", scatter_dimension=1, tiled=True)
    grad_inner_raw = nt(cot_all, down_units)
    grad_logit = (
        jnp.sum(inner[:, routed:] * grad_inner_raw[:, routed:], axis=1, keepdims=True)
        * switch_gate
        * (1.0 - switch_gate)
    )
    grad_inner = grad_inner_raw * share
    slope = logistic * (1.0 + gate_act * (1.0 - logistic))
    grad_gate_act = (grad_inner * up_act * slope).astype(BF16)
    grad_up_act = (grad_inner * silu).astype(BF16)
    back_two = nn(grad_gate_act, gate_units) + nn(grad_up_act, up_units)
    back_two = (back_two + grad_logit * switch.astype(F32)).astype(BF16)
    back_two = scatter_all(back_two).astype(F32)
    grad_down = tn(inner_share, cot_all)
    grad_gate = tn(grad_gate_act, normed_two)
    grad_up = tn(grad_up_act, normed_two)
    grad_switch = jnp.sum(grad_logit * normed_two.astype(F32), axis=0)
    sent_back = jnp.stack([grad_gate, grad_up, grad_down]).astype(BF16)
    sent_back = sent_back.reshape(3, units, n_dp, slice_d).transpose(2, 0, 1, 3)
    returned = exchange_dp(sent_back).astype(F32)

    def split_units(value):
        routed_part = value[:, :routed].reshape(experts, expert_cols, slice_d)
        return (routed_part, value[:, routed:].reshape(shared_cols, slice_d))

    grad_gate_experts, grad_gate_shared = split_units(returned[:, 0])
    grad_up_experts, grad_up_shared = split_units(returned[:, 1])
    grad_down_experts, grad_down_shared = split_units(returned[:, 2])
    unused_two, norm_two_back = jax.vjp(normalize, middle, gain_two)
    grad_middle_norm, grad_gain_two = norm_two_back(back_two)
    grad_middle = own_rows(cot).astype(F32) + grad_middle_norm
    grad_attn = lax.all_gather(grad_middle.astype(BF16), "tensor", axis=0, tiled=True)
    grad_weight_o = tn(grad_attn, attended)
    grad_attended = nn(grad_attn, weight_o).astype(BF16).reshape(head_shape)
    grad_values = (
        jnp.einsum("bhqk,bqhd->bkhd", probs_low, grad_attended, preferred_element_type=F32)
        .astype(BF16)
        .reshape(rows, -1)
    )
    grad_probs = jnp.einsum("bqhd,bkhd->bhqk", grad_attended, values, preferred_element_type=F32)
    grad_scores = (
        probs * (grad_probs - jnp.sum(grad_probs * probs, axis=-1, keepdims=True))
    ).astype(BF16)
    grad_queries = (
        (jnp.einsum("bhqk,bkhd->bqhd", grad_scores, keys, preferred_element_type=F32) * scale)
        .astype(BF16)
        .reshape(rows, -1)
    )
    grad_keys = (
        (jnp.einsum("bhqk,bqhd->bkhd", grad_scores, queries, preferred_element_type=F32) * scale)
        .astype(BF16)
        .reshape(rows, -1)
    )
    grad_qkv = jnp.concatenate([grad_queries, grad_keys, grad_values], axis=1)
    grad_attn_weights = jnp.concatenate([tn(normed_one, grad_qkv), grad_weight_o], axis=1).astype(
        BF16
    )
    grad_attn_weights = lax.psum_scatter(
        grad_attn_weights, "dp", scatter_dimension=0, tiled=True
    ).astype(F32)
    back_one = nt(grad_qkv, weight_qkv)
    back_one = lax.psum_scatter(back_one, "tensor", scatter_dimension=0, tiled=True)
    unused_one, norm_one_back = jax.vjp(normalize, inputs_own, gain_one)
    grad_input_norm, grad_gain_one = norm_one_back(back_one)
    grad_input = grad_middle + grad_input_norm
    bias_part = jnp.concatenate(
        [
            jnp.sum(grad_queries.astype(F32), axis=0).reshape(heads, n_dp, piece),
            jnp.sum(grad_values.astype(F32), axis=0).reshape(heads, n_dp, piece),
        ],
        axis=0,
    )
    bias_part = bias_part.transpose(1, 0, 2).reshape(1, n_dp, -1)
    mine = (jnp.arange(n_tensor) == member)[:, None, None]
    bias_part = jnp.where(mine, bias_part, 0.0)
    gains = jnp.concatenate([grad_gain_one, grad_gain_two, grad_switch])
    gains = gains.reshape(1, 3, n_dp, slice_d).transpose(0, 2, 1, 3).reshape(n_dp, 3 * slice_d)
    pack = jnp.concatenate([gains, bias_part.transpose(1, 0, 2).reshape(n_dp, -1)], axis=1)
    pack = lax.psum(pack, ALL)
    pack = lax.dynamic_slice_in_dim(pack, place, 1, 0)[0]
    bias_own = lax.dynamic_slice_in_dim(
        pack[3 * slice_d :].reshape(n_tensor, 2, heads, piece), member, 1, 0
    )[0]

    def to_columns(value):
        return lax.all_to_all(value, "tensor", 1, 0, tiled=True)

    out_shape = (seqs, span, width // n_tensor)
    output = jnp.where(valid, to_columns(middle) + mixed.astype(F32), 0.0).reshape(out_shape)
    tokens_grad = jnp.where(valid, to_columns(grad_input), 0.0).reshape(out_shape)
    return (
        output,
        tokens_grad,
        pack[:slice_d],
        grad_attn_weights[:, :head_cols],
        bias_own[0],
        grad_attn_weights[:, head_cols : 2 * head_cols],
        grad_attn_weights[:, 2 * head_cols : 3 * head_cols],
        bias_own[1],
        grad_attn_weights[:, 3 * head_cols :].T,
        pack[slice_d : 2 * slice_d],
        grad_gate_experts.transpose(0, 2, 1),
        grad_up_experts.transpose(0, 2, 1),
        grad_down_experts,
        grad_gate_shared.T,
        grad_up_shared.T,
        grad_down_shared,
        pack[2 * slice_d : 3 * slice_d],
    )


IN_SPECS = (
    P("dp", None, None),
    P("dp", None, None),
    P("dp", None, None),
    P("dp", None, None),
    P("dp"),
    P(),
    P("dp"),
    P("dp", "tensor"),
    P("tensor", "dp"),
    P("dp", "tensor"),
    P("dp", "tensor"),
    P("tensor", "dp"),
    P("tensor", "dp"),
    P("dp"),
    P(None, "dp", "tensor"),
    P(None, "dp", "tensor"),
    P(None, "tensor", "dp"),
    P("dp", "tensor"),
    P("dp", "tensor"),
    P("tensor", "dp"),
    P("dp"),
)
OUT_SPECS = (P("dp", None, "tensor"), P("dp", None, "tensor")) + IN_SPECS[6:]


def solution(mesh):
    return jax.shard_map(
        per_device, mesh=mesh, in_specs=IN_SPECS, out_specs=OUT_SPECS, check_vma=False
    )
```

profile of v0, /device:TPU:0, one launch (start us, length us, event | category | flops | bytes accessed | tf_op | source)
XLA Modules:
  0.0 1104.9 jit_solution(10503144483082694511)
XLA Ops:
  13.3 33.5 %all-gather = bf16[8,1,896]{2,1,0:T(2,128)(2,1)S(1)} all-gather(bf16[1,1,896]{2,1,0:T(2,128)(2,1)S(1)} %bitcast.258), channel_id=1, replica_groups=mesh['dp'=8,'tensor'=4] {'dp'}, dimensions={0}, use_global_device_ids=true | all-gather | bytes 16128 | tf_op jit(solution)/shard_map/all_gather | solution.py:93
  49.2 91.7 %all-gather.6.cloned.1.call-done = bf16[2048,2048]{0,1:T(8,128)(2,1)} async-done(((bf16[256,2048]{0,1:T(8,128)(2,1)}), bf16[2048,2048]{0,1:T(8,128)(2,1)}) %all-gather.6.cloned.1.call-update) | async-done | bytes 8388624 | tf_op jit(solution)/shard_map/all_gather | solution.py:114
  140.9 4.6 fusion.7
  149.5 3.6 fusion.18
  156.4 26.3 %reduce-scatter.7.cloned.1.call-done = f32[64,2048]{1,0:T(8,128)} async-done(((f32[256,2048]{1,0:T(8,128)}), f32[64,2048]{1,0:T(8,128)}) %reduce-scatter.7.cloned.1.call-update) | async-done | bytes 524304 | tf_op jit(solution)/shard_map/reduce_scatter | solution.py:162
  182.7 1.9 multiply_reduce_fusion.6
  185.5 2.5 copy.155
  188.0 2.5 copy.156
  197.4 3.0 pad_maximum_fusion.1
  200.5 5.5 all-to-all-start.1
  206.3 145.4 %all-to-all-done.1 = bf16[8,3,440,256]{3,2,1,0:T(8,128)(2,1)} async-done(((bf16[8,3,440,256]{3,2,1,0:T(8,128)(2,1)}), bf16[8,3,440,256]{3,2,1,0:T(8,128)(2,1)}, u32[]{:S(2)}, u32[]{:S(2)}) %all-to-all-start.1) | async-done | bytes 5406752 | tf_op jit(solution)/shard_map/all_to_all | solution.py:41
  351.7 2.9 fusion.66
  359.0 2.9 fusion.40
  361.9 44.5 %all-gather.8.cloned.1.call-done = bf16[2048,2048]{1,0:T(8,128)(2,1)} async-done(((bf16[64,2048]{1,0:T(8,128)(2,1)}), bf16[2048,2048]{1,0:T(8,128)(2,1)}) %all-gather.8.cloned.1.call-update) | async-done | bytes 8388624 | tf_op jit(solution)/shard_map/all_gather | solution.py:33
  406.4 5.8 fusion.73
  412.6 5.7 fusion.72
  418.3 5.8 fusion.71
  424.3 11.5 %multiply_convert_fusion = (bf16[2048,440]{0,1:T(8,128)(2,1)}, bf16[2048,440]{0,1:T(8,128)(2,1)S(1)}, bf16[2048,440]{0,1:T(8,128)(2,1)}, f32[2048,440]{0,1:T(8,128)}, f32[2048,440]{0,1:T(8,128)}) fusion(f32[2048,176]{0,1:T(8,128)S(1)} %broadcast_in_dim.169, f32[2048,264]{0,1:T(8,128)S(1)} %copy-done.11, f32[2048,440]{0,1:T(8,128)} %fusion.71, ...), kind=kOutput, calls=%fused_computation.24 | convolution fusion | flops 3709009920 | bytes 33619968 | tf_op jit(solution)/shard_map/dot_general | solution.py:21
  435.8 2.6 fusion.21
  438.5 8.2 fusion.74
  446.6 11.2 %add_convert_fusion = bf16[2048,2048]{1,0:T(8,128)(2,1)} fusion(f32[2048,2048]{1,0:T(8,128)} %fusion.74, f32[2048]{0:T(1024)S(1)} %convert_element_type.270, f32[2048]{0:T(1024)S(1)} %subtract_multiply_fusion, bf16[2048,440]{0,1:T(8,128)(2,1)} %get-tuple-element.98, bf16[440,2048]{1,0:T(8,128)(2,1)S(1)} %bitcast.231), kind=kOutput, calls=%fused_computation.2 | convolution fusion | flops 3707764736 | bytes 28786688 | tf_op jit(solution)/shard_map/dot_general | solution.py:29
  458.4 9.9 convolution_convert_fusion.1
  468.3 138.6 %reduce-scatter.13.cloned.1.call-done = bf16[64,2048]{1,0:T(8,128)(2,1)} async-done(((bf16[2048,2048]{1,0:T(8,128)(2,1)}), bf16[64,2048]{1,0:T(8,128)(2,1)}) %reduce-scatter.13.cloned.1.call-update) | async-done | bytes 262160 | tf_op jit(solution)/shard_map/reduce_scatter | solution.py:37
  608.1 1.9 fusion.64
  610.1 143.7 %reduce-scatter.9.cloned.1.call-done = bf16[256,2048]{1,0:T(8,128)(2,1)} async-done(((bf16[2048,2048]{1,0:T(8,128)(2,1)}), bf16[256,2048]{1,0:T(8,128)(2,1)}) %reduce-scatter.9.cloned.1.call-update) | async-done | bytes 1048592 | tf_op jit(solution)/shard_map/reduce_scatter | solution.py:184
  753.8 3.4 fusion.25
  762.4 2.3 convert_reduce_fusion
  767.8 6.2 fusion.5
  774.2 3.4 convolution_convert_fusion.2
  777.6 4.5 convolution_convert_fusion
  782.2 8.4 pad_maximum_fusion
  790.6 7.8 fusion.13
  800.8 7.5 convolution_convert_fusion.4
  810.3 4.1 convolution_convert_fusion.3
  815.4 2.9 maximum_bitcast_fusion
  818.3 4.9 all-to-all-start.3
  824.1 5.1 multiply_reduce_fusion
  829.2 179.2 %all-to-all-done.3 = bf16[8,3,440,256]{3,2,1,0:T(8,128)(2,1)} async-done(((bf16[8,3,440,256]{3,2,1,0:T(8,128)(2,1)}), bf16[8,3,440,256]{3,2,1,0:T(8,128)(2,1)}, u32[]{:S(2)}, u32[]{:S(2)}) %all-to-all-start.3) | async-done | bytes 5406752 | tf_op jit(solution)/shard_map/all_to_all | solution.py:41
  1008.4 3.5 all-to-all-start
  1011.9 3.5 copy_convert_fusion
  1015.4 4.2 slice_bitcast_fusion
  1019.6 2.6 slice.224
  1022.2 3.2 slice.221
  1032.7 2.9 copy.181
  1035.6 3.0 copy.180
  1038.9 1.9 fusion.44
  1044.7 3.5 all-to-all-start.2
  1048.2 41.3 %psum.7 = f32[8,1280]{1,0:T(8,128)S(1)} all-reduce(f32[8,1280]{1,0:T(8,128)S(1)} %pad_maximum_fusion.4), channel_id=1, replica_groups=mesh['dp'=8,'tensor'=4] {'dp','tensor'}, use_global_device_ids=true, to_apply=%region_19.20 | all-reduce | flops 10240 | bytes 81920 | tf_op jit(solution)/shard_map/psum | solution.py:264
  (228 shorter events, 63.0 us)
Async XLA Ops:
  8.0 3.6 copy-start.21
  8.0 132.9 %all-gather.6.cloned.1.call-start = ((), (), s32[]{:S(2)}) async-start(), calls=%async_computation.10 | async-start | bytes 9437184 | tf_op jit(solution)/shard_map/all_gather | solution.py:114
  11.7 35.6 %copy-start.4 = (bf16[2,128,2048]{2,1,0:T(8,128)(2,1)S(1)}, bf16[2,128,2048]{2,1,0:T(8,128)(2,1)}, u32[]{:S(2)}) copy-start(bf16[2,128,2048]{2,1,0:T(8,128)(2,1)} %param.21) | copy-start | bytes 3145732
  12.8 169.9 %reduce-scatter.7.cloned.1.call-start = ((), (), s32[]{:S(2)}) async-start(), calls=%async_computation.11 | async-start | bytes 2621440 | tf_op jit(solution)/shard_map/reduce_scatter | solution.py:162
  46.9 2.3 copy-start.23
  145.6 3.3 copy-start.19
  147.8 1.5 copy-start.22
  148.0 5.2 copy-start.12
  149.5 3.8 copy-start.36
  149.5 4.3 copy-start.25
  149.5 4.3 copy-start.26
  153.2 205.8 %all-gather.10.cloned.1.call-start = ((), (), s32[]{:S(2)}) async-start(), calls=%async_computation.13 | async-start | bytes 9191424 | tf_op jit(solution)/shard_map/all_gather | solution.py:33
  153.8 28.9 %copy-start.27 = (pred[256]{0:T(512)(128)(4,1)}, pred[256]{0:T(512)(128)(4,1)S(1)}, u32[]{:S(2)}) copy-start(pred[256]{0:T(512)(128)(4,1)S(1)} %get-tuple-element.131) | copy-start | bytes 772
  156.4 250.0 %all-gather.8.cloned.1.call-start = ((), (), s32[]{:S(2)}) async-start(), calls=%async_computation.12 | async-start | bytes 8650752 | tf_op jit(solution)/shard_map/all_gather | solution.py:33
  190.5 2.1 copy-start.8
  192.5 1.6 copy-start.9
  194.1 1.6 copy-start.10
  200.5 151.3 %all-to-all-start.1 = ((bf16[8,3,440,256]{3,2,1,0:T(8,128)(2,1)}), bf16[8,3,440,256]{3,2,1,0:T(8,128)(2,1)}, u32[]{:S(2)}, u32[]{:S(2)}) async-start(bf16[8,3,440,256]{3,2,1,0:T(8,128)(2,1)} %pad_maximum_fusion.1), calls=%async_computation.2 | async-start | bytes 10813440 | tf_op jit(solution)/shard_map/all_to_all | solution.py:41
  206.0 400.9 %reduce-scatter.13.cloned.1.call-start = ((), (), s32[]{:S(2)}) async-start(), calls=%async_computation.16 | async-start | bytes 8650752 | tf_op jit(solution)/shard_map/reduce_scatter | solution.py:37
  406.4 5.8 copy-start
  406.4 6.3 copy-start.15
  412.6 5.7 copy-start.16
  418.3 6.0 copy-start.11
  418.3 6.0 copy-start.14
  435.8 10.8 copy-start.37
  457.9 295.8 %reduce-scatter.9.cloned.1.call-start = ((), (), s32[]{:S(2)}) async-start(), calls=%async_computation.14 | async-start | bytes 9437184 | tf_op jit(solution)/shard_map/reduce_scatter | solution.py:184
  468.3 285.6 %all-gather.12.cloned.1.call-start = ((), (), s32[]{:S(2)}) async-start(), calls=%async_computation.17 | async-start | bytes 1310720 | tf_op jit(solution)/shard_map/all_gather | solution.py:217
  610.0 428.9 %reduce-scatter.11.cloned.1.call-start = ((), (), s32[]{:S(2)}) async-start(), calls=%async_computation.15 | async-start | bytes 1310720 | tf_op jit(solution)/shard_map/reduce_scatter | solution.py:185
  753.8 287.0 %reduce-scatter.15.cloned.1.call-start = ((), (), s32[]{:S(2)}) async-start(), calls=%async_computation.18 | async-start | bytes 2621440 | tf_op jit(solution)/shard_map/reduce_scatter | solution.py:247
  758.9 1.7 copy-start.13
  758.9 2.3 copy-start.20
  774.0 317.8 %reduce-scatter.17.cloned.1.call-start = ((), (), s32[]{:S(2)}) async-start(), calls=%async_computation.19 | async-start | bytes 9437184 | tf_op jit(solution)/shard_map/reduce_scatter | solution.py:243
  774.2 3.4 copy-start.18
  798.4 10.8 slice-start
  799.0 1.8 copy-start.38
  800.8 8.4 slice-start.1
  808.8 1.5 copy-start.39
  818.3 5.8 copy-start.31
  818.3 190.1 %all-to-all-start.3 = ((bf16[8,3,440,256]{3,2,1,0:T(8,128)(2,1)}), bf16[8,3,440,256]{3,2,1,0:T(8,128)(2,1)}, u32[]{:S(2)}, u32[]{:S(2)}) async-start(bf16[8,3,440,256]{3,2,1,0:T(8,128)(2,1)} %maximum_bitcast_fusion), calls=%async_computation.9 | async-start | bytes 10813440 | tf_op jit(solution)/shard_map/all_to_all | solution.py:41
  1008.4 30.5 %all-to-all-start = ((f32[64,4,512]{2,0,1:T(8,128)}), f32[64,4,512]{2,0,1:T(8,128)S(1)}, u32[]{:S(2)}, u32[]{:S(2)}) async-start(f32[64,4,512]{2,0,1:T(8,128)} %bitcast.197), calls=%async_computation.1 | async-start | bytes 1048576 | tf_op jit(solution)/shard_map/all_to_all | solution.py:271
  1022.2 3.2 copy-start.2
  1026.7 3.3 copy-start.1
  1035.6 3.3 copy-start.28
  1035.6 5.2 copy-start.24
  1035.6 6.7 copy-start.7
  1042.3 48.6 %copy-start.32 = (pred[2,128]{1,0:T(4,128)(4,1)S(1)}, pred[2,128]{1,0:T(4,128)(4,1)}, u32[]{:S(2)}) copy-start(pred[2,128]{1,0:T(4,128)(4,1)} %get-tuple-element.130) | copy-start | bytes 772
  1044.7 46.2 %all-to-all-start.2 = ((f32[64,4,512]{2,0,1:T(8,128)}), f32[64,4,512]{2,0,1:T(8,128)S(1)}, u32[]{:S(2)}, u32[]{:S(2)}) async-start(f32[64,4,512]{2,0,1:T(8,128)} %bitcast.196), calls=%async_computation.7 | async-start | bytes 1048576 | tf_op jit(solution)/shard_map/all_to_all | solution.py:271
  1093.1 3.0 copy-start.3
  (8 other events, 9.7 us)
Sparse Core Ops, SparseCore 0:
  13.0 127.8 all-gather.5
  153.3 29.3 reduce-scatter.6
  610.1 12.5 all-gather.11
  753.9 23.8 reduce-scatter.10
  780.2 31.1 reduce-scatter.14
  814.9 251.4 reduce-scatter.16
Sparse Core Ops, SparseCore 1:
  157.1 113.9 all-gather.9
  274.4 131.9 all-gather.7
  458.0 148.8 reduce-scatter.12
  610.5 143.2 reduce-scatter.8
where the time goes:
time: 1110 us; the launch traced here: 1100 us
  waiting for transfers between devices  770 us (69%)
  matrix products  111 us (10%)
  blocking collectives  74.8 us (7%)
  local copies, waits for them, and re-layouts  66.3 us (6%)
  other arithmetic  47.6 us (4%)
  starting transfers between devices  18.5 us (2%)
  between operations  16.9 us (2%)
    all_to_all x2, waiting for transfers between devices, exchange_dp(): return lax.all_to_all(value, 'dp', 0, 0, tiled=False)  325 us
    reduce_scatter x1, waiting for transfers between devices, per_device(): mixed = lax.psum_scatter(mixed, 'dp', scatter_dimension=0, tiled=True)  144 us
    reduce_scatter x1, waiting for transfers between devices, scatter_all(): return lax.psum_scatter(value, ALL, scatter_dimension=0, tiled=True)  139 us
    all_gather x1, waiting for transfers between devices, per_device(): attn_weights = lax.all_gather(attn_weights, 'dp', axis=0, tiled=True)  91.7 us
    all_gather x2, waiting for transfers between devices, gather_all(): return lax.all_gather(value, ALL, axis=0, tiled=True)  44.5 us
    psum x1, blocking collectives, per_device(): pack = lax.psum(pack, ALL)  41.3 us
    dot_general x6, matrix products, nn(): lax.dot_general(left, right, (((1,), (0,)), ((), ())), preferred_element_...  40.1 us
    dot_general x6, matrix products, nt(): lax.dot_general(left, right, (((1,), (1,)), ((), ())), preferred_element_...  38.7 us
  transfers between devices with their start and end apart: 14, of which 7 were waited for; matrix products, arithmetic and copies ran while one was open for 13% of the time, Pallas kernels for 0%

commit v1 on v0

--- a/solution.py
+++ b/solution.py
@@ -3,6 +3,7 @@
 import jax.numpy as jnp
 from jax import lax
 from jax.sharding import PartitionSpec as P
+from jax.lax import all_gather
 
 HEAD_DIM = 128
 EPSILON = 1e-06
@@ -261,7 +262,11 @@
     gains = jnp.concatenate([grad_gain_one, grad_gain_two, grad_switch])
     gains = gains.reshape(1, 3, n_dp, slice_d).transpose(0, 2, 1, 3).reshape(n_dp, 3 * slice_d)
     pack = jnp.concatenate([gains, bias_part.transpose(1, 0, 2).reshape(n_dp, -1)], axis=1)
-    pack = lax.psum(pack, ALL)
+
+    def sample_feed(base_x, ax_name):
+        return all_gather(base_x, axis_name=ax_name).sum(axis=0)
+
+    pack = sample_feed(pack, ALL)
     pack = lax.dynamic_slice_in_dim(pack, place, 1, 0)[0]
     bias_own = lax.dynamic_slice_in_dim(
         pack[3 * slice_d :].reshape(n_tensor, 2, heads, piece), member, 1, 0

time: 1110 us -> 1100 us (level)
  blocking collectives: 74.8 us -> 33.5 us
  waiting for transfers between devices: 770 us -> 808 us
  local copies, waits for them, and re-layouts: 66.3 us -> 50.7 us
    psum x1 -> x0, blocking collectives: 41.3 us -> none  [per_device(): pack = lax.psum(pack, ALL)]
    reduce_scatter x1, waiting for transfers between devices: 0.01 us -> 27.8 us  [per_device(): lax.psum_scatter(back_one, 'tensor', scatter_dimension=0, tiled=True)]
    unnamed x107 -> x131, local copies, waits for them, and re-layouts: 35 us -> 28.1 us
  transfers between devices with their start and end apart: 14 -> 15, of which waited for: 7 -> 10; matrix products, arithmetic and copies ran while one was open for 13% -> 12% of each run, Pallas kernels for 0% -> 0%
where the time goes in v1:
time: 1100 us; the launch traced here: 1090 us
  waiting for transfers between devices  808 us (73%)
  matrix products  107 us (10%)
  other arithmetic  52.7 us (5%)
  local copies, waits for them, and re-layouts  50.7 us (5%)
  blocking collectives  33.5 us (3%)
  starting transfers between devices  20 us (2%)
  between operations  17.3 us (2%)
    all_to_all x2, waiting for transfers between devices, exchange_dp(): return lax.all_to_all(value, 'dp', 0, 0, tiled=False)  322 us
    reduce_scatter x1, waiting for transfers between devices, scatter_all(): return lax.psum_scatter(value, ALL, scatter_dimension=0, tiled=True)  149 us
    reduce_scatter x1, waiting for transfers between devices, per_device(): mixed = lax.psum_scatter(mixed, 'dp', scatter_dimension=0, tiled=True)  139 us
    all_gather x1, waiting for transfers between devices, per_device(): attn_weights = lax.all_gather(attn_weights, 'dp', axis=0, tiled=True)  91.1 us
    all_gather x2, waiting for transfers between devices, gather_all(): return lax.all_gather(value, ALL, axis=0, tiled=True)  43.7 us
    dot_general x6, matrix products, nn(): lax.dot_general(left, right, (((1,), (0,)), ((), ())), preferred_element_...  39 us
    dot_general x6, matrix products, nt(): lax.dot_general(left, right, (((1,), (1,)), ((), ())), preferred_element_...  38.5 us
    all_gather x1, blocking collectives, per_device(): small = lax.all_gather(small[None, :], 'dp', axis=0, tiled=True)  33.5 us
  transfers between devices with their start and end apart: 15, of which 10 were waited for; matrix products, arithmetic and copies ran while one was open for 12% of the time, Pallas kernels for 0%

profile of v1, /device:TPU:0, one launch (start us, length us, event | category | flops | bytes accessed | tf_op | source)
XLA Modules:
  0.0 1089.5 jit_solution(3765501444707938096)
XLA Ops:
  13.3 33.5 %all-gather.1 = bf16[8,1,896]{2,1,0:T(2,128)(2,1)S(1)} all-gather(bf16[1,1,896]{2,1,0:T(2,128)(2,1)S(1)} %bitcast.259), channel_id=1, replica_groups=mesh['dp'=8,'tensor'=4] {'dp'}, dimensions={0}, use_global_device_ids=true | all-gather | bytes 16128 | tf_op jit(solution)/shard_map/all_gather | solution.py:94
  48.2 1.6 multiply_convert_fusion.3
  49.8 91.1 %all-gather.8.cloned.1.call-done = bf16[2048,2048]{0,1:T(8,128)(2,1)} async-done(((bf16[256,2048]{0,1:T(8,128)(2,1)}), bf16[2048,2048]{0,1:T(8,128)(2,1)}) %all-gather.8.cloned.1.call-update) | async-done | bytes 8388624 | tf_op jit(solution)/shard_map/all_gather | solution.py:115
  140.9 4.6 fusion.7
  147.9 3.6 fusion.18
  153.9 27.2 %reduce-scatter.7.cloned.1.call-done = f32[64,2048]{1,0:T(8,128)} async-done(((f32[256,2048]{1,0:T(8,128)}), f32[64,2048]{1,0:T(8,128)}) %reduce-scatter.7.cloned.1.call-update) | async-done | bytes 524304 | tf_op jit(solution)/shard_map/reduce_scatter | solution.py:163
  181.1 1.9 multiply_reduce_fusion.6
  183.9 1.6 copy.193
  185.5 1.6 copy.194
  192.9 3.0 pad_maximum_fusion.1
  196.0 5.7 all-to-all-start.1
  202.6 147.5 %all-to-all-done.1 = bf16[8,3,440,256]{3,2,1,0:T(8,128)(2,1)} async-done(((bf16[8,3,440,256]{3,2,1,0:T(8,128)(2,1)}), bf16[8,3,440,256]{3,2,1,0:T(8,128)(2,1)}, u32[]{:S(2)}, u32[]{:S(2)}) %all-to-all-start.1) | async-done | bytes 5406752 | tf_op jit(solution)/shard_map/all_to_all | solution.py:42
  350.1 2.9 fusion.66
  357.4 2.9 fusion.40
  360.3 43.7 %all-gather.10.cloned.1.call-done = bf16[2048,2048]{1,0:T(8,128)(2,1)} async-done(((bf16[64,2048]{1,0:T(8,128)(2,1)}), bf16[2048,2048]{1,0:T(8,128)(2,1)}) %all-gather.10.cloned.1.call-update) | async-done | bytes 8388624 | tf_op jit(solution)/shard_map/all_gather | solution.py:34
  403.9 5.8 fusion.73
  410.2 5.7 fusion.72
  415.9 5.8 fusion.71
  421.8 11.4 %multiply_convert_fusion = (bf16[2048,440]{0,1:T(8,128)(2,1)}, bf16[2048,440]{0,1:T(8,128)(2,1)}, bf16[2048,440]{0,1:T(8,128)(2,1)}, f32[2048,440]{0,1:T(8,128)S(1)}, f32[2048,440]{0,1:T(8,128)}) fusion(f32[2048,176]{0,1:T(8,128)S(1)} %broadcast_in_dim.169, f32[2048,264]{0,1:T(8,128)S(1)} %copy-done.9, f32[2048,440]{0,1:T(8,128)} %fusion.71, ...), kind=kOutput, calls=%fused_computation.24 | convolution fusion | flops 3709009920 | bytes 33619968 | tf_op jit(solution)/shard_map/dot_general | solution.py:22
  433.2 1.7 fusion.21
  435.2 8.2 fusion.74
  443.3 10.8 add_convert_fusion
  454.2 148.8 %reduce-scatter.13.cloned.1.call-done = bf16[64,2048]{1,0:T(8,128)(2,1)} async-done(((bf16[2048,2048]{1,0:T(8,128)(2,1)}), bf16[64,2048]{1,0:T(8,128)(2,1)}) %reduce-scatter.13.cloned.1.call-update) | async-done | bytes 262160 | tf_op jit(solution)/shard_map/reduce_scatter | solution.py:38
  604.2 1.9 fusion.64
  606.3 10.0 convolution_convert_fusion.1
  616.4 2.4 all-gather.14.cloned.1.call-done
  618.8 2.7 fusion.25
  624.9 6.2 fusion.5
  631.2 138.6 %reduce-scatter.9.cloned.1.call-done = bf16[256,2048]{1,0:T(8,128)(2,1)} async-done(((bf16[2048,2048]{1,0:T(8,128)(2,1)}), bf16[256,2048]{1,0:T(8,128)(2,1)}) %reduce-scatter.9.cloned.1.call-update) | async-done | bytes 1048592 | tf_op jit(solution)/shard_map/reduce_scatter | solution.py:185
  770.0 5.1 multiply_reduce_fusion
  775.4 27.8 %reduce-scatter.15.cloned.1.call-done = f32[64,2048]{1,0:T(8,128)} async-done(((f32[256,2048]{1,0:T(8,128)}), f32[64,2048]{1,0:T(8,128)}) %reduce-scatter.15.cloned.1.call-update) | async-done | bytes 524304 | tf_op jit(solution)/shard_map/reduce_scatter | solution.py:248
  805.5 2.0 convolution_convert_fusion.2
  807.5 6.0 convolution_convert_fusion
  813.5 7.8 pad_maximum_fusion
  822.7 7.3 fusion.13
  832.4 7.4 convolution_convert_fusion.4
  840.8 1.6 copy-done.51
  842.4 4.2 convolution_convert_fusion.3
  847.5 3.0 maximum_bitcast_fusion
  850.5 5.6 all-to-all-start.3
  856.9 174.2 %all-to-all-done.3 = bf16[8,3,440,256]{3,2,1,0:T(8,128)(2,1)} async-done(((bf16[8,3,440,256]{3,2,1,0:T(8,128)(2,1)}), bf16[8,3,440,256]{3,2,1,0:T(8,128)(2,1)}, u32[]{:S(2)}, u32[]{:S(2)}) %all-to-all-start.3) | async-done | bytes 5406752 | tf_op jit(solution)/shard_map/all_to_all | solution.py:42
  1031.1 3.5 all-to-all-start
  1034.7 7.7 copy_convert_fusion
  1044.7 4.1 all-to-all-start.2
  1048.8 5.0 slice_bitcast_fusion
  1062.9 1.9 fusion.44
  1064.8 2.0 broadcast_select_fusion
  1069.6 6.7 reduce-scatter.17.cloned.1.call-done
  (255 shorter events, 57.2 us)
Async XLA Ops:
  8.0 3.6 copy-start.20
  8.0 132.9 %all-gather.8.cloned.1.call-start = ((), (), s32[]{:S(2)}) async-start(), calls=%async_computation.10 | async-start | bytes 9437184 | tf_op jit(solution)/shard_map/all_gather | solution.py:115
  11.7 36.2 %copy-start.4 = (bf16[2,128,2048]{2,1,0:T(8,128)(2,1)S(1)}, bf16[2,128,2048]{2,1,0:T(8,128)(2,1)}, u32[]{:S(2)}) copy-start(bf16[2,128,2048]{2,1,0:T(8,128)(2,1)} %param.21) | copy-start | bytes 3145732
  12.8 168.2 %reduce-scatter.7.cloned.1.call-start = ((), (), s32[]{:S(2)}) async-start(), calls=%async_computation.11 | async-start | bytes 2621440 | tf_op jit(solution)/shard_map/reduce_scatter | solution.py:163
  49.8 95.7 %copy-start.3 = (bf16[256,2048]{1,0:T(8,128)(2,1)}, bf16[256,2048]{1,0:T(8,128)(2,1)S(1)}, u32[]{:S(2)}) copy-start(bf16[256,2048]{1,0:T(8,128)(2,1)S(1)} %get-tuple-element.110) | copy-start | bytes 3145732
  146.4 5.2 copy-start.11
  147.3 4.2 copy-start.23
  147.9 3.8 copy-start.46
  147.9 4.3 copy-start.28
  147.9 4.3 copy-start.32
  151.6 205.8 %all-gather.12.cloned.1.call-start = ((), (), s32[]{:S(2)}) async-start(), calls=%async_computation.13 | async-start | bytes 9191424 | tf_op jit(solution)/shard_map/all_gather | solution.py:34
  152.2 30.8 %copy-start.33 = (pred[256]{0:T(512)(128)(4,1)}, pred[256]{0:T(512)(128)(4,1)S(1)}, u32[]{:S(2)}) copy-start(pred[256]{0:T(512)(128)(4,1)S(1)} %get-tuple-element.148) | copy-start | bytes 772
  153.0 451.2 %copy-start.2 = (bf16[256,2048]{1,0:T(8,128)(2,1)}, bf16[256,2048]{1,0:T(8,128)(2,1)S(1)}, u32[]{:S(2)}) copy-start(bf16[256,2048]{1,0:T(8,128)(2,1)S(1)} %bitcast_select_fusion) | copy-start | bytes 3145732
  153.8 250.1 %all-gather.10.cloned.1.call-start = ((), (), s32[]{:S(2)}) async-start(), calls=%async_computation.12 | async-start | bytes 8650752 | tf_op jit(solution)/shard_map/all_gather | solution.py:34
  195.9 6.0 copy-start.26
  196.0 6.6 copy-start.25
  196.0 154.1 %all-to-all-start.1 = ((bf16[8,3,440,256]{3,2,1,0:T(8,128)(2,1)}), bf16[8,3,440,256]{3,2,1,0:T(8,128)(2,1)}, u32[]{:S(2)}, u32[]{:S(2)}) async-start(bf16[8,3,440,256]{3,2,1,0:T(8,128)(2,1)} %pad_maximum_fusion.1), calls=%async_computation.2 | async-start | bytes 10813440 | tf_op jit(solution)/shard_map/all_to_all | solution.py:42
  201.7 401.3 %reduce-scatter.13.cloned.1.call-start = ((), (), s32[]{:S(2)}) async-start(), calls=%async_computation.16 | async-start | bytes 8650752 | tf_op jit(solution)/shard_map/reduce_scatter | solution.py:38
  403.9 5.8 copy-start
  403.9 6.3 copy-start.14
  410.2 5.7 copy-start.15
  415.9 5.9 copy-start.9
  415.9 5.9 copy-start.13
  435.2 8.2 copy-start.27
  435.2 8.2 copy-start.50
  454.1 148.8 %copy-start.30 = (f32[64]{0:T(128)S(1)}, f32[64]{0:T(128)}, u32[]{:S(2)}) copy-start(f32[64]{0:T(128)} %copy-done.29) | copy-start | bytes 772
  454.1 150.1 %copy-start.41 = (f32[64]{0:T(128)S(1)}, f32[64]{0:T(128)}, u32[]{:S(2)}) copy-start(f32[64]{0:T(128)} %copy-done.40) | copy-start | bytes 772
  454.1 164.7 %all-gather.14.cloned.1.call-start = ((), (), s32[]{:S(2)}) async-start(), calls=%async_computation.17 | async-start | bytes 1310720 | tf_op jit(solution)/shard_map/all_gather | solution.py:218
  604.2 12.1 %copy-start.35 = (f32[64]{0:T(128)}, f32[64]{0:T(128)S(1)}, u32[]{:S(2)}) copy-start(f32[64]{0:T(128)S(1)} %multiply_multiply_fusion.1) | copy-start | bytes 772
  606.1 163.7 %reduce-scatter.9.cloned.1.call-start = ((), (), s32[]{:S(2)}) async-start(), calls=%async_computation.14 | async-start | bytes 9437184 | tf_op jit(solution)/shard_map/reduce_scatter | solution.py:185
  616.3 5.3 copy-start.12
  616.3 5.3 copy-start.22
  616.4 5.3 copy-start.24
  616.4 186.8 %reduce-scatter.15.cloned.1.call-start = ((), (), s32[]{:S(2)}) async-start(), calls=%async_computation.18 | async-start | bytes 2621440 | tf_op jit(solution)/shard_map/reduce_scatter | solution.py:248
  624.9 6.2 copy-start.16
  631.1 138.9 %copy-start.39 = (f32[64]{0:T(128)S(1)}, f32[64]{0:T(128)}, u32[]{:S(2)}) copy-start(f32[64]{0:T(128)} %get-tuple-element.122) | copy-start | bytes 772
  631.1 431.8 %reduce-scatter.11.cloned.1.call-start = ((), (), s32[]{:S(2)}) async-start(), calls=%async_computation.15 | async-start | bytes 1310720 | tf_op jit(solution)/shard_map/reduce_scatter | solution.py:186
  769.8 296.9 %all-gather.16.cloned.1.call-start = ((), (), s32[]{:S(2)}) async-start(), calls=%async_computation.20 | async-start | bytes 1351680 | tf_op jit(solution)/shard_map/all_gather | solution.py:267
  805.3 271.0 %reduce-scatter.17.cloned.1.call-start = ((), (), s32[]{:S(2)}) async-start(), calls=%async_computation.19 | async-start | bytes 9437184 | tf_op jit(solution)/shard_map/reduce_scatter | solution.py:244
  830.0 10.8 slice-start
  832.4 8.4 slice-start.1
  850.5 180.6 %all-to-all-start.3 = ((bf16[8,3,440,256]{3,2,1,0:T(8,128)(2,1)}), bf16[8,3,440,256]{3,2,1,0:T(8,128)(2,1)}, u32[]{:S(2)}, u32[]{:S(2)}) async-start(bf16[8,3,440,256]{3,2,1,0:T(8,128)(2,1)} %maximum_bitcast_fusion), calls=%async_computation.9 | async-start | bytes 10813440 | tf_op jit(solution)/shard_map/all_to_all | solution.py:42
  1031.1 13.6 %all-to-all-start = ((f32[64,4,512]{2,0,1:T(8,128)}), f32[64,4,512]{2,0,1:T(8,128)S(1)}, u32[]{:S(2)}, u32[]{:S(2)}) async-start(f32[64,4,512]{2,0,1:T(8,128)} %bitcast.199), calls=%async_computation.1 | async-start | bytes 1048576 | tf_op jit(solution)/shard_map/all_to_all | solution.py:276
  1034.6 7.7 copy-start.5
  1034.6 7.7 copy-start.10
  1034.6 7.7 copy-start.31
  1034.6 7.7 copy-start.36
  1044.7 20.1 %all-to-all-start.2 = ((f32[64,4,512]{2,0,1:T(8,128)}), f32[64,4,512]{2,0,1:T(8,128)}, u32[]{:S(2)}, u32[]{:S(2)}) async-start(f32[64,4,512]{2,0,1:T(8,128)} %bitcast.198), calls=%async_computation.7 | async-start | bytes 1048576 | tf_op jit(solution)/shard_map/all_to_all | solution.py:276
  (21 other events, 34.0 us)
Sparse Core Ops, SparseCore 0:
  13.0 127.8 all-gather.7
  151.7 29.3 reduce-scatter.6
  606.2 12.5 all-gather.13
  622.3 147.4 reduce-scatter.8
  772.8 30.2 reduce-scatter.14
  805.5 24.7 reduce-scatter.10
  833.9 242.2 reduce-scatter.16
Sparse Core Ops, SparseCore 1:
  155.5 114.0 all-gather.11
  272.9 131.0 all-gather.9
  454.2 148.7 reduce-scatter.12
  805.3 89.9 all-gather.15
